TPU v7x, 128 devices: a whole 4x4x4 slice. The times are simulated.
128 devices in a mesh: ep: 8 (over y, core), fs: 16 (over z, x).
Axes of the slice: x: 4, y: 4, z: 4, core: 2. Of those that a mesh axis runs over, the one named last changes fastest.
Arguments:
- grads: bfloat16 [8, 8, 256, 14336], P('ep', None, 'fs'), may hold values from -64 to 64
- counts: int32 [8, 8], replicated, may hold values from 16 to 2047
- weight: bfloat16 [8, 256, 14336], P('ep', 'fs'), may hold values from -3 to 3
- mom: float32 [8, 256, 14336], P('ep', 'fs'), may hold values from -64 to 64
- second: float32 [8, 256, 14336], P('ep', 'fs'), may hold values from 0.1 to 10
- in_weight: float32 [6, 32], replicated, may hold values from -2.5 to 2.5
- in_bias: float32 [32], replicated, may hold values from -3 to 3
- out_weight: float32 [32, 2], replicated, may hold values from -1 to 1
- out_bias: float32 [2], replicated, may hold values from -3 to 3
Outputs:
- new_weight: bfloat16 [8, 256, 14336], P('ep')
- new_mom: float32 [8, 256, 14336], P('ep', 'fs')
- new_second: float32 [8, 256, 14336], P('ep', 'fs')
All inputs are finite; a program needn't handle non-finite values.
Results may differ from a plain program's by a relative error of at most 0.0019.
Values may be sent and summed in bfloat16 or wider, within the bound.
A program may use at most 64 MiB of HBM per device.

v0:
```python
import jax
import jax.numpy as jnp
from jax import lax
from jax.sharding import PartitionSpec as P

MOMENTUM_DECAY = 0.9
SECOND_DECAY = 0.99
NORM_EPS = 1e-06
ROOT_EPS = 1e-08
STEP_SCALE = 0.2
EXP_SCALE = 0.5


def from_everyone(value, axis):
    copies = jnp.broadcast_to(value, (lax.axis_size(axis), *value.shape))
    return lax.all_to_all(copies, axis, split_axis=0, concat_axis=0, tiled=True)


def of_everyone(value, axis):
    return from_everyone(value, axis).sum(axis=0)


def in_one(arrays, axis):
    line, at, done = (jnp.concatenate([a.reshape(-1) for a in arrays]), 0, [])
    so_far = of_everyone(line, axis)
    for a in arrays:
        done.append(so_far[at : at + a.size].reshape(a.shape))
        at += a.size
    return tuple(done)


def learned_step(
    gradient,
    mom_next,
    second_next,
    weight,
    grad_norm,
    mom_norm,
    in_weight,
    in_bias,
    out_weight,
    out_bias,
):
    inv_root = lax.rsqrt(second_next + ROOT_EPS)
    features = jnp.stack(
        [
            gradient / grad_norm,
            mom_next / mom_norm,
            mom_next * inv_root,
            gradient * inv_root,
            weight.astype(jnp.float32),
            jnp.broadcast_to(jnp.log(mom_norm), gradient.shape),
        ]
    )
    hidden = jax.nn.relu(
        jnp.einsum("fh,fab->hab", in_weight, features, precision=lax.Precision.HIGHEST)
        + in_bias[:, None, None]
    )
    outputs = (
        jnp.einsum("hk,hab->kab", out_weight, hidden, precision=lax.Precision.HIGHEST)
        + out_bias[:, None, None]
    )
    update = STEP_SCALE * outputs[0] * jnp.exp(EXP_SCALE * outputs[1])
    return (weight.astype(jnp.float32) - update).astype(jnp.bfloat16)


def add_sources(arrived):
    return jnp.sum(arrived.astype(jnp.float32), axis=0)


def per_device(grads, counts, weight, mom, second, in_weight, in_bias, out_weight, out_bias):
    source = lax.axis_index("ep")
    counts_f = counts.astype(jnp.float32)
    totals = jnp.sum(counts_f, axis=0)
    share_row = lax.dynamic_index_in_dim(counts_f, source, 0, keepdims=False) / totals
    weighted = share_row[None, :, None, None] * grads.astype(jnp.float32)
    outgoing = weighted.astype(jnp.bfloat16)
    gradient = add_sources(lax.all_to_all(outgoing, "ep", split_axis=1, concat_axis=0, tiled=True))[
        0
    ]
    mom_here = mom[0]
    second_here = second[0]
    mom_next = MOMENTUM_DECAY * mom_here + (1.0 - MOMENTUM_DECAY) * gradient
    second_next = SECOND_DECAY * second_here + (1.0 - SECOND_DECAY) * gradient * gradient
    entries = gradient.shape[0] * gradient.shape[1] * lax.axis_size("fs")
    grad_sq, mom_sq = in_one((jnp.sum(gradient * gradient), jnp.sum(mom_next * mom_next)), "fs")
    grad_norm = jnp.sqrt(grad_sq / entries + NORM_EPS)
    mom_norm = jnp.sqrt(mom_sq / entries + NORM_EPS)
    width = gradient.shape[1]

    def block_step(items):
        grad_block, mom_block, second_block, weight_block = items
        return learned_step(
            grad_block,
            mom_block,
            second_block,
            weight_block,
            grad_norm,
            mom_norm,
            in_weight,
            in_bias,
            out_weight,
            out_bias,
        )

    blocks = lax.map(
        block_step,
        (
            gradient.reshape(-1, 2, width),
            mom_next.reshape(-1, 2, width),
            second_next.reshape(-1, 2, width),
            weight[0].reshape(-1, 2, width),
        ),
    )
    updated = blocks.reshape(gradient.shape)
    gathered = lax.all_gather(updated[None], "fs", axis=1, tiled=True)
    return (gathered, mom_next[None], second_next[None])


def solution(mesh):
    in_specs = (
        P("ep", None, "fs", None),
        P(),
        P("ep", "fs", None),
        P("ep", "fs", None),
        P("ep", "fs", None),
        P(),
        P(),
        P(),
        P(),
    )
    out_specs = (P("ep", None, None), P("ep", "fs", None), P("ep", "fs", None))
    return jax.shard_map(
        per_device, mesh=mesh, in_specs=in_specs, out_specs=out_specs, check_vma=False
    )
```

profile of v0, /device:TPU:1, one launch (start us, length us, event | category | flops | bytes accessed | tf_op | source)
XLA Modules:
  0.0 246.2 jit_solution(12678078749305325285)
XLA Ops:
  7.2 0.7 convert_reduce_fusion.1
  7.9 0.7 convert_element_type.34
  8.6 4.7 %multiply_convert_fusion = bf16[1,8,16,14336]{3,2,0,1:T(8,128)(2,1)} fusion(bf16[1,8,16,14336]{3,2,1,0:T(8,128)(2,1)} %param.11, f32[8]{0:T(128)S(1)} %bitcast_divide_fusion), kind=kLoop, calls=%fused_computation.22 | loop fusion | flops 5505024 | bytes 7340064 | tf_op jit(solution)/shard_map/convert_element_type | solution.py:77
  13.3 6.1 %all-to-all-start = ((bf16[1,8,16,14336]{3,2,0,1:T(8,128)(2,1)}), bf16[1,8,16,14336]{3,2,0,1:T(8,128)(2,1)}, u32[]{:S(2)}, u32[]{:S(2)}) async-start(bf16[1,8,16,14336]{3,2,0,1:T(8,128)(2,1)} %multiply_convert_fusion), calls=%async_computation | async-start | bytes 7340032 | tf_op jit(solution)/shard_map/all_to_all | solution.py:78
  19.7 42.8 %all-to-all-done = bf16[1,8,16,14336]{3,2,0,1:T(8,128)(2,1)} async-done(((bf16[1,8,16,14336]{3,2,0,1:T(8,128)(2,1)}), bf16[1,8,16,14336]{3,2,0,1:T(8,128)(2,1)}, u32[]{:S(2)}, u32[]{:S(2)}) %all-to-all-start) | async-done | bytes 3670048 | tf_op jit(solution)/shard_map/all_to_all | solution.py:78
  62.5 2.6 %convert_reduce_fusion = f32[16,14336]{1,0:T(8,128)S(1)} fusion(bf16[1,8,16,14336]{3,2,0,1:T(8,128)(2,1)} %all-to-all-done), kind=kLoop, calls=%fused_computation.21 | loop fusion | flops 3440640 | bytes 4587520 | tf_op jit(solution)/shard_map/reduce_sum | solution.py:68
  65.1 1.5 reshape_squeeze.7
  66.6 0.9 multiply_reduce_fusion
  67.5 1.4 pad_maximum_fusion
  68.8 0.6 broadcast_in_dim.18
  69.5 7.6 %all-to-all-start.1 = ((f32[16,1,2]{2,1,0:T(1,128)}), f32[16,1,2]{2,1,0:T(1,128)S(1)}, u32[]{:S(2)}, u32[]{:S(2)}) async-start(f32[16,1,2]{2,1,0:T(1,128)} %broadcast_in_dim.18), calls=%async_computation.1 | async-start | bytes 16384 | tf_op jit(solution)/shard_map/all_to_all | solution.py:16
  77.3 2.9 %fusion.10 = (f32[1,16,14336]{2,1,0:T(8,128)}, f32[1,16,14336]{2,1,0:T(8,128)}, f32[1,16,14336]{2,1,0:T(8,128)}, f32[1,16,14336]{2,1,0:T(8,128)S(1)}) fusion(f32[16,14336]{1,0:T(8,128)S(1)} %convert_reduce_fusion, f32[1,16,14336]{2,1,0:T(8,128)} %param.15, f32[1,16,14336]{2,1,0:T(8,128)S(1)} %copy-done), kind=kLoop, calls=%fused_computation.26 | loop fusion | flops 1605632 | bytes 6422528 | tf_op jit(solution)/shard_map/add | solution.py:84
  80.2 1.7 mul.131
  81.9 0.5 mul.126
  82.5 4.1 %fusion.9 = (f32[8,2,14336]{2,0,1:T(8,128)S(1)}, f32[8,2,14336]{2,0,1:T(8,128)}, f32[8,2,14336]{2,0,1:T(8,128)}) fusion(f32[8,2,14336]{2,1,0:T(2,128)S(1)} %mul.131, f32[8,2,14336]{2,1,0:T(2,128)} %reshape_squeeze.7, f32[8,2,14336]{2,1,0:T(2,128)S(1)} %mul.126), kind=kLoop, calls=%fused_computation.25 | loop fusion | flops 1146880 | bytes 5505024 | tf_op jit(solution)/shard_map/add | solution.py:84
  86.6 0.6 fusion.14
  88.4 75.6 %while.11 = (s32[]{:T(128)}, bf16[8,2,14336]{2,1,0:T(2,128)(2,1)}, bf16[8,2,14336]{2,1,0:T(2,128)(2,1)S(1)}, f32[8,2,14336]{2,0,1:T(8,128)}, f32[]{:T(128)}, /*i...) while((s32[]{:T(128)}, bf16[8,2,14336]{2,1,0:T(2,128)(2,1)}, ...), condition=%wide.region_6.7_spmd, body=%wide.region_5.6_spmd.sunk | while | flops 90316800 | bytes 11298093 | solution.py:106
  88.7 1.8 dynamic-slice_multiply_fusion.3
  90.5 1.1 stack.4
  91.6 3.2 %fusion.28 = f32[32,2,14336]{2,0,1:T(8,128)S(1)} fusion(f32[6,2,14336]{2,0,1:T(8,128)S(1)} %stack.4, f32[32]{0:T(128)S(1)} %get-tuple-element.350, f32[6,32]{1,0:T(8,128)S(1)} %get-tuple-element.349), kind=kOutput, calls=%fused_computation.2.clone.1 | convolution fusion | flops 67895296 | bytes 4359040 | tf_op jit(solution)/shard_map/while/body/eval_jaxpr/fh,fab->hab/dot_general | solution.py:56
  94.8 2.1 fusion.29
  96.9 0.3 fusion.30
  97.2 0.7 copy_dynamic-update-slice_fusion.2
  98.1 1.8 dynamic-slice_multiply_fusion.3
  99.9 1.1 stack.4
  101.1 3.2 %fusion.28 = f32[32,2,14336]{2,0,1:T(8,128)S(1)} fusion(f32[6,2,14336]{2,0,1:T(8,128)S(1)} %stack.4, f32[32]{0:T(128)S(1)} %get-tuple-element.350, f32[6,32]{1,0:T(8,128)S(1)} %get-tuple-element.349), kind=kOutput, calls=%fused_computation.2.clone.1 | convolution fusion | flops 67895296 | bytes 4359040 | tf_op jit(solution)/shard_map/while/body/eval_jaxpr/fh,fab->hab/dot_general | solution.py:56
  104.3 2.1 fusion.29
  106.3 0.3 fusion.30
  106.7 0.7 copy_dynamic-update-slice_fusion.2
  107.6 1.8 dynamic-slice_multiply_fusion.3
  109.4 1.1 stack.4
  110.5 3.2 %fusion.28 = f32[32,2,14336]{2,0,1:T(8,128)S(1)} fusion(f32[6,2,14336]{2,0,1:T(8,128)S(1)} %stack.4, f32[32]{0:T(128)S(1)} %get-tuple-element.350, f32[6,32]{1,0:T(8,128)S(1)} %get-tuple-element.349), kind=kOutput, calls=%fused_computation.2.clone.1 | convolution fusion | flops 67895296 | bytes 4359040 | tf_op jit(solution)/shard_map/while/body/eval_jaxpr/fh,fab->hab/dot_general | solution.py:56
  113.7 2.1 fusion.29
  115.8 0.3 fusion.30
  116.1 0.7 copy_dynamic-update-slice_fusion.2
  117.0 1.8 dynamic-slice_multiply_fusion.3
  118.8 1.1 stack.4
  120.0 3.2 %fusion.28 = f32[32,2,14336]{2,0,1:T(8,128)S(1)} fusion(f32[6,2,14336]{2,0,1:T(8,128)S(1)} %stack.4, f32[32]{0:T(128)S(1)} %get-tuple-element.350, f32[6,32]{1,0:T(8,128)S(1)} %get-tuple-element.349), kind=kOutput, calls=%fused_computation.2.clone.1 | convolution fusion | flops 67895296 | bytes 4359040 | tf_op jit(solution)/shard_map/while/body/eval_jaxpr/fh,fab->hab/dot_general | solution.py:56
  123.2 2.1 fusion.29
  125.2 0.3 fusion.30
  125.5 0.7 copy_dynamic-update-slice_fusion.2
  126.4 1.8 dynamic-slice_multiply_fusion.3
  128.3 1.1 stack.4
  129.4 3.2 %fusion.28 = f32[32,2,14336]{2,0,1:T(8,128)S(1)} fusion(f32[6,2,14336]{2,0,1:T(8,128)S(1)} %stack.4, f32[32]{0:T(128)S(1)} %get-tuple-element.350, f32[6,32]{1,0:T(8,128)S(1)} %get-tuple-element.349), kind=kOutput, calls=%fused_computation.2.clone.1 | convolution fusion | flops 67895296 | bytes 4359040 | tf_op jit(solution)/shard_map/while/body/eval_jaxpr/fh,fab->hab/dot_general | solution.py:56
  132.6 2.1 fusion.29
  135.0 0.7 copy_dynamic-update-slice_fusion.2
  135.9 1.8 dynamic-slice_multiply_fusion.3
  137.7 1.1 stack.4
  138.9 3.2 %fusion.28 = f32[32,2,14336]{2,0,1:T(8,128)S(1)} fusion(f32[6,2,14336]{2,0,1:T(8,128)S(1)} %stack.4, f32[32]{0:T(128)S(1)} %get-tuple-element.350, f32[6,32]{1,0:T(8,128)S(1)} %get-tuple-element.349), kind=kOutput, calls=%fused_computation.2.clone.1 | convolution fusion | flops 67895296 | bytes 4359040 | tf_op jit(solution)/shard_map/while/body/eval_jaxpr/fh,fab->hab/dot_general | solution.py:56
  142.1 2.1 fusion.29
  144.4 0.7 copy_dynamic-update-slice_fusion.2
  145.3 1.8 dynamic-slice_multiply_fusion.3
  147.2 1.1 stack.4
  148.3 3.2 %fusion.28 = f32[32,2,14336]{2,0,1:T(8,128)S(1)} fusion(f32[6,2,14336]{2,0,1:T(8,128)S(1)} %stack.4, f32[32]{0:T(128)S(1)} %get-tuple-element.350, f32[6,32]{1,0:T(8,128)S(1)} %get-tuple-element.349), kind=kOutput, calls=%fused_computation.2.clone.1 | convolution fusion | flops 67895296 | bytes 4359040 | tf_op jit(solution)/shard_map/while/body/eval_jaxpr/fh,fab->hab/dot_general | solution.py:56
  151.5 2.1 fusion.29
  153.9 0.7 copy_dynamic-update-slice_fusion.2
  154.8 1.8 dynamic-slice_multiply_fusion.3
  156.6 1.1 stack.4
  157.8 3.2 %fusion.28 = f32[32,2,14336]{2,0,1:T(8,128)S(1)} fusion(f32[6,2,14336]{2,0,1:T(8,128)S(1)} %stack.4, f32[32]{0:T(128)S(1)} %get-tuple-element.350, f32[6,32]{1,0:T(8,128)S(1)} %get-tuple-element.349), kind=kOutput, calls=%fused_computation.2.clone.1 | convolution fusion | flops 67895296 | bytes 4359040 | tf_op jit(solution)/shard_map/while/body/eval_jaxpr/fh,fab->hab/dot_general | solution.py:56
  161.0 2.1 fusion.29
  163.3 0.7 copy_dynamic-update-slice_fusion.2
  164.0 2.0 broadcast_in_dim_reshape.3
  166.0 66.5 %all-gather.2.cloned.1.call-done = bf16[1,256,14336]{2,1,0:T(8,128)(2,1)} async-done(((bf16[1,16,14336]{2,1,0:T(8,128)(2,1)}), bf16[1,256,14336]{2,1,0:T(8,128)(2,1)}) %all-gather.2.cloned.1.call-update) | async-done | bytes 7340048 | tf_op jit(solution)/shard_map/all_gather | solution.py:116
  232.5 6.9 %copy.86 = bf16[1,256,14336]{2,1,0:T(8,128)(2,1)} copy(bf16[1,256,14336]{2,1,0:T(8,128)(2,1)} %all-gather.2.cloned.1.call-done) | data formatting | bytes 14680064
  (47 shorter events, 3.4 us)
Async XLA Ops:
  13.2 6.1 %copy-start.1 = (bf16[1,16,14336]{2,1,0:T(8,128)(2,1)S(1)}, bf16[1,16,14336]{2,1,0:T(8,128)(2,1)}, u32[]{:S(2)}) copy-start(bf16[1,16,14336]{2,1,0:T(8,128)(2,1)} %param.13) | copy-start | bytes 1376260
  13.3 49.3 %all-to-all-start = ((bf16[1,8,16,14336]{3,2,0,1:T(8,128)(2,1)}), bf16[1,8,16,14336]{3,2,0,1:T(8,128)(2,1)}, u32[]{:S(2)}, u32[]{:S(2)}) async-start(bf16[1,8,16,14336]{3,2,0,1:T(8,128)(2,1)} %multiply_convert_fusion), calls=%async_computation | async-start | bytes 7340032 | tf_op jit(solution)/shard_map/all_to_all | solution.py:78
  19.3 47.3 %copy-start = (f32[1,16,14336]{2,1,0:T(8,128)S(1)}, f32[1,16,14336]{2,1,0:T(8,128)}, u32[]{:S(2)}) copy-start(f32[1,16,14336]{2,1,0:T(8,128)} %param.14) | copy-start | bytes 2752516
  69.5 17.1 %all-to-all-start.1 = ((f32[16,1,2]{2,1,0:T(1,128)}), f32[16,1,2]{2,1,0:T(1,128)S(1)}, u32[]{:S(2)}, u32[]{:S(2)}) async-start(f32[16,1,2]{2,1,0:T(1,128)} %broadcast_in_dim.18), calls=%async_computation.1 | async-start | bytes 16384 | tf_op jit(solution)/shard_map/all_to_all | solution.py:16
  77.1 155.4 %all-gather.2.cloned.1.call-start = ((), (), s32[]{:S(2)}) async-start(), calls=%async_computation.2 | async-start | bytes 7798784 | tf_op jit(solution)/shard_map/all_gather | solution.py:116
  81.9 6.5 %copy-start.2 = (f32[6,32]{1,0:T(8,128)S(1)}, f32[6,32]{1,0:T(8,128)}, u32[]{:S(2)}) copy-start(f32[6,32]{1,0:T(8,128)} %param.16) | copy-start | bytes 2308
  81.9 6.5 %copy-start.3 = (f32[32,2]{0,1:T(2,128)S(1)}, f32[32,2]{0,1:T(2,128)}, u32[]{:S(2)}) copy-start(f32[32,2]{0,1:T(2,128)} %param.18) | copy-start | bytes 772
  81.9 6.5 %copy-start.4 = (f32[32]{0:T(128)S(1)}, f32[32]{0:T(128)}, u32[]{:S(2)}) copy-start(f32[32]{0:T(128)} %param.17) | copy-start | bytes 388
  81.9 6.5 %copy-start.5 = (f32[2]{0:T(128)S(1)}, f32[2]{0:T(128)}, u32[]{:S(2)}) copy-start(f32[2]{0:T(128)} %param.19) | copy-start | bytes 28
Sparse Core Ops, SparseCore 0:
  166.1 66.3 all-gather.1
where the time goes:
time: 247 us; the launch traced here: 246 us
  waiting for transfers between devices  109 us (44%)
  matrix products  42 us (17%)
  other arithmetic  35.8 us (14%)
  local copies, waits for them, and re-layouts  29.4 us (12%)
  between operations  15.4 us (6%)
  starting transfers between devices  13.9 us (6%)
    all_gather x1, waiting for transfers between devices, per_device(): gathered = lax.all_gather(updated[None], 'fs', axis=1, tiled=True)  66.5 us
    all_to_all x1, waiting for transfers between devices, per_device(): lax.all_to_all(outgoing, 'ep', split_axis=1, concat_axis=0, tiled=True)  42.8 us
    dot_general x8, matrix products, learned_step(): jnp.einsum('fh,fab->hab', in_weight, features, precision=lax.Precision.HI...  25.6 us
    dot_general x8, matrix products, learned_step(): jnp.einsum('hk,hab->kab', out_weight, hidden, precision=lax.Precision.HIG...  16.4 us
    mul x8, other arithmetic, learned_step(): gradient * inv_root  14.7 us
    another operation x8, local copies, waits for them, and re-layouts, learned_step(): jnp.stack([gradient / grad_norm, mom_next / mom_norm, mom_next * inv_root...  8.98 us
    all_to_all x1, starting transfers between devices, from_everyone(): return lax.all_to_all(copies, axis, split_axis=0, concat_axis=0, tiled=True)  7.6 us
    unnamed x13, local copies, waits for them, and re-layouts  6.93 us
  transfers between devices with their start and end apart: 3, of which 2 were waited for; matrix products, arithmetic and copies ran while one was open for 4% of the time, Pallas kernels for 0%

commit v1 on v0

--- a/solution.py
+++ b/solution.py
@@ -113,7 +113,11 @@
         ),
     )
     updated = blocks.reshape(gradient.shape)
-    gathered = lax.all_gather(updated[None], "fs", axis=1, tiled=True)
+    count = lax.axis_size("fs")
+    repeats = [count if d == 1 else 1 for d in range(updated[None].ndim)]
+    gathered = lax.all_to_all(
+        jnp.tile(updated[None], repeats), "fs", split_axis=1, concat_axis=1, tiled=True
+    )
     return (gathered, mom_next[None], second_next[None])
 
 

time: 247 us -> 401 us (1.62)
  local copies, waits for them, and re-layouts: 29.4 us -> 126 us
  blocking collectives: 0 us -> 90.3 us
  waiting for transfers between devices: 109 us -> 42.9 us
  other arithmetic: 35.8 us -> 80.9 us
  between operations: 15.4 us -> 2.21 us
    all_to_all x0 -> x1, blocking collectives: none -> 90.3 us  [per_device(): lax.all_to_all(jnp.tile(updated[None], repeats), 'fs', split_axis=1, conc...]
    all_gather x1 -> x0, waiting for transfers between devices: 66.5 us -> none  [per_device(): gathered = lax.all_gather(updated[None], 'fs', axis=1, tiled=True)]
    another operation x1 -> x3, local copies, waits for them, and re-layouts: 1.96 us -> 62.6 us  [per_device(): jnp.tile(updated[None], repeats)]
    unnamed x0 -> x1, other arithmetic: none -> 45.1 us
    unnamed x13 -> x18, local copies, waits for them, and re-layouts: 6.93 us -> 42 us
  transfers between devices with their start and end apart: 3 -> 2, of which waited for: 2 -> 1; matrix products, arithmetic and copies ran while one was open for 4% -> 3% of each run, Pallas kernels for 0% -> 0%
where the time goes in v1:
time: 401 us; the launch traced here: 398 us
  local copies, waits for them, and re-layouts  126 us (31%)
  blocking collectives  90.3 us (23%)
  other arithmetic  80.9 us (20%)
  waiting for transfers between devices  42.9 us (11%)
  matrix products  42 us (10%)
  starting transfers between devices  13.7 us (3%)
    all_to_all x1, blocking collectives, per_device(): lax.all_to_all(jnp.tile(updated[None], repeats), 'fs', split_axis=1, conc...  90.3 us
    another operation x3, local copies, waits for them, and re-layouts, per_device(): jnp.tile(updated[None], repeats)  62.6 us
    unnamed x1, other arithmetic  45.1 us
    all_to_all x1, waiting for transfers between devices, per_device(): lax.all_to_all(outgoing, 'ep', split_axis=1, concat_axis=0, tiled=True)  42.8 us
    unnamed x18, local copies, waits for them, and re-layouts  42 us
    dot_general x8, matrix products, learned_step(): jnp.einsum('fh,fab->hab', in_weight, features, precision=lax.Precision.HI...  25.6 us
    dot_general x8, matrix products, learned_step(): jnp.einsum('hk,hab->kab', out_weight, hidden, precision=lax.Precision.HIG...  16.4 us
    mul x8, other arithmetic, learned_step(): gradient * inv_root  14.7 us
  transfers between devices with their start and end apart: 2, of which 1 were waited for; matrix products, arithmetic and copies ran while one was open for 3% of the time, Pallas kernels for 0%

profile of v1, /device:TPU:1, one launch (start us, length us, event | category | flops | bytes accessed | tf_op | source)
XLA Modules:
  0.0 398.4 jit_solution(5473966493798060428)
XLA Ops:
  0.6 0.7 convert_reduce_fusion.1
  1.3 0.7 convert_element_type.34
  2.0 4.7 %multiply_convert_fusion = bf16[1,8,16,14336]{3,2,0,1:T(8,128)(2,1)} fusion(bf16[1,8,16,14336]{3,2,1,0:T(8,128)(2,1)} %param.11, f32[8]{0:T(128)S(1)} %bitcast_divide_fusion), kind=kLoop, calls=%fused_computation.22 | loop fusion | flops 5505024 | bytes 7340064 | tf_op jit(solution)/shard_map/convert_element_type | solution.py:77
  6.7 6.1 %all-to-all-start = ((bf16[1,8,16,14336]{3,2,0,1:T(8,128)(2,1)}), bf16[1,8,16,14336]{3,2,0,1:T(8,128)(2,1)}, u32[]{:S(2)}, u32[]{:S(2)}) async-start(bf16[1,8,16,14336]{3,2,0,1:T(8,128)(2,1)} %multiply_convert_fusion), calls=%async_computation | async-start | bytes 7340032 | tf_op jit(solution)/shard_map/all_to_all | solution.py:78
  13.1 42.8 %all-to-all-done = bf16[1,8,16,14336]{3,2,0,1:T(8,128)(2,1)} async-done(((bf16[1,8,16,14336]{3,2,0,1:T(8,128)(2,1)}), bf16[1,8,16,14336]{3,2,0,1:T(8,128)(2,1)}, u32[]{:S(2)}, u32[]{:S(2)}) %all-to-all-start) | async-done | bytes 3670048 | tf_op jit(solution)/shard_map/all_to_all | solution.py:78
  56.0 2.6 convert_reduce_fusion
  58.6 1.5 reshape_squeeze.7
  60.1 0.9 multiply_reduce_fusion
  60.9 1.4 pad_maximum_fusion
  62.3 0.6 broadcast_in_dim.18
  62.9 7.6 %all-to-all-start.1 = ((f32[16,1,2]{2,1,0:T(1,128)}), f32[16,1,2]{2,1,0:T(1,128)S(1)}, u32[]{:S(2)}, u32[]{:S(2)}) async-start(f32[16,1,2]{2,1,0:T(1,128)} %broadcast_in_dim.18), calls=%async_computation.1 | async-start | bytes 16384 | tf_op jit(solution)/shard_map/all_to_all | solution.py:16
  70.5 2.9 fusion.10
  73.4 1.8 mul.131
  75.2 1.5 mul.126
  76.7 4.1 %fusion.9 = (f32[8,2,14336]{2,0,1:T(8,128)S(1)}, f32[8,2,14336]{2,0,1:T(8,128)}, f32[8,2,14336]{2,0,1:T(8,128)}) fusion(f32[8,2,14336]{2,1,0:T(2,128)S(1)} %mul.131, f32[8,2,14336]{2,1,0:T(2,128)S(1)} %copy-done.1, f32[8,2,14336]{2,1,0:T(2,128)} %mul.126), kind=kLoop, calls=%fused_computation.25 | loop fusion | flops 1146880 | bytes 5505024 | tf_op jit(solution)/shard_map/add | solution.py:84
  82.9 75.6 %while.11 = (s32[]{:T(128)}, bf16[8,2,14336]{2,1,0:T(2,128)(2,1)}, bf16[8,2,14336]{2,1,0:T(2,128)(2,1)S(1)}, f32[8,2,14336]{2,0,1:T(8,128)}, f32[]{:T(128)}, /*i...) while((s32[]{:T(128)}, bf16[8,2,14336]{2,1,0:T(2,128)(2,1)}, ...), condition=%wide.region_6.7_spmd, body=%wide.region_5.6_spmd.sunk | while | flops 90316800 | bytes 11298093 | solution.py:106
  83.1 1.8 dynamic-slice_multiply_fusion.3
  85.0 1.1 stack.4
  86.1 3.2 fusion.28
  89.3 2.1 fusion.29
  91.7 0.7 copy_dynamic-update-slice_fusion.2
  92.6 1.8 dynamic-slice_multiply_fusion.3
  94.4 1.1 stack.4
  95.6 3.2 fusion.28
  98.8 2.1 fusion.29
  101.1 0.7 copy_dynamic-update-slice_fusion.2
  102.0 1.8 dynamic-slice_multiply_fusion.3
  103.9 1.1 stack.4
  105.0 3.2 fusion.28
  108.2 2.1 fusion.29
  110.6 0.7 copy_dynamic-update-slice_fusion.2
  111.5 1.8 dynamic-slice_multiply_fusion.3
  113.3 1.1 stack.4
  114.5 3.2 fusion.28
  117.7 2.1 fusion.29
  120.0 0.7 copy_dynamic-update-slice_fusion.2
  120.9 1.8 dynamic-slice_multiply_fusion.3
  122.8 1.1 stack.4
  123.9 3.2 fusion.28
  127.1 2.1 fusion.29
  129.5 0.7 copy_dynamic-update-slice_fusion.2
  130.4 1.8 dynamic-slice_multiply_fusion.3
  132.2 1.1 stack.4
  133.4 3.2 fusion.28
  136.6 2.1 fusion.29
  138.9 0.7 copy_dynamic-update-slice_fusion.2
  139.8 1.8 dynamic-slice_multiply_fusion.3
  141.7 1.1 stack.4
  142.8 3.2 fusion.28
  146.0 2.1 fusion.29
  148.4 0.7 copy_dynamic-update-slice_fusion.2
  149.3 1.8 dynamic-slice_multiply_fusion.3
  151.1 1.1 stack.4
  152.2 3.2 fusion.28
  155.5 2.1 fusion.29
  157.8 0.7 copy_dynamic-update-slice_fusion.2
  158.5 1.2 tile.10
  159.7 0.8 tile.11
  160.5 60.5 %copy.86 = bf16[1,256,14336]{2,0,1:T(2,128)(2,1)} copy(bf16[1,256,14336]{2,1,0:T(8,128)(2,1)S(1)} %bitcast.51) | data formatting | bytes 14680064 | tf_op jit(solution)/shard_map/tile | solution.py:119
  221.7 45.1 %reduce.3 = bf16[256,14336]{1,0:T(8,128)(2,1)} reduce(bf16[256,1,14336]{2,1,0:T(2,128)(2,1)} %bitcast.49, bf16[]{:T(256)} %broadcast.67), dimensions={1}, to_apply=%bitcast.36.reduce_sub_computation | reduce | bytes 14680066
  266.8 13.7 %reshape.100 = bf16[16,2,114688]{2,1,0:T(2,128)(2,1)} reshape(bf16[256,14336]{1,0:T(8,128)(2,1)} %reduce.3) | data formatting | bytes 14680064
  280.5 90.3 %all_to_all.20 = bf16[16,2,114688]{2,1,0:T(2,128)(2,1)} all-to-all(bf16[16,2,114688]{2,1,0:T(2,128)(2,1)} %reshape.100), channel_id=1, replica_groups=mesh['ep'=8,'fs'=16] {'fs'}, dimensions={0} | all-to-all | bytes 14680064 | tf_op jit(solution)/shard_map/all_to_all | solution.py:118
  370.7 15.3 %reshape.101 = bf16[256,1,14336]{2,1,0:T(2,128)(2,1)} reshape(bf16[16,2,114688]{2,1,0:T(2,128)(2,1)} %all_to_all.20) | data formatting | bytes 14680064
  386.1 12.4 %copy.69 = bf16[1,256,14336]{2,1,0:T(8,128)(2,1)} copy(bf16[1,256,14336]{2,0,1:T(2,128)(2,1)} %bitcast.50) | data formatting | bytes 14680064
  (53 shorter events, 5.6 us)
Async XLA Ops:
  6.7 6.1 %copy-start.2 = (bf16[1,16,14336]{2,1,0:T(8,128)(2,1)S(1)}, bf16[1,16,14336]{2,1,0:T(8,128)(2,1)}, u32[]{:S(2)}) copy-start(bf16[1,16,14336]{2,1,0:T(8,128)(2,1)} %param.13) | copy-start | bytes 1376260
  6.7 49.3 %all-to-all-start = ((bf16[1,8,16,14336]{3,2,0,1:T(8,128)(2,1)}), bf16[1,8,16,14336]{3,2,0,1:T(8,128)(2,1)}, u32[]{:S(2)}, u32[]{:S(2)}) async-start(bf16[1,8,16,14336]{3,2,0,1:T(8,128)(2,1)} %multiply_convert_fusion), calls=%async_computation | async-start | bytes 7340032 | tf_op jit(solution)/shard_map/all_to_all | solution.py:78
  12.8 47.3 %copy-start = (f32[1,16,14336]{2,1,0:T(8,128)S(1)}, f32[1,16,14336]{2,1,0:T(8,128)}, u32[]{:S(2)}) copy-start(f32[1,16,14336]{2,1,0:T(8,128)} %param.14) | copy-start | bytes 2752516
  62.9 17.9 %all-to-all-start.1 = ((f32[16,1,2]{2,1,0:T(1,128)}), f32[16,1,2]{2,1,0:T(1,128)S(1)}, u32[]{:S(2)}, u32[]{:S(2)}) async-start(f32[16,1,2]{2,1,0:T(1,128)} %broadcast_in_dim.18), calls=%async_computation.1 | async-start | bytes 16384 | tf_op jit(solution)/shard_map/all_to_all | solution.py:16
  73.4 3.3 copy-start.1
  75.2 7.7 %copy-start.3 = (f32[6,32]{1,0:T(8,128)S(1)}, f32[6,32]{1,0:T(8,128)}, u32[]{:S(2)}) copy-start(f32[6,32]{1,0:T(8,128)} %param.16) | copy-start | bytes 2308
  75.2 7.7 %copy-start.4 = (f32[32,2]{0,1:T(2,128)S(1)}, f32[32,2]{0,1:T(2,128)}, u32[]{:S(2)}) copy-start(f32[32,2]{0,1:T(2,128)} %param.18) | copy-start | bytes 772
  75.2 7.7 %copy-start.5 = (f32[32]{0:T(128)S(1)}, f32[32]{0:T(128)}, u32[]{:S(2)}) copy-start(f32[32]{0:T(128)} %param.17) | copy-start | bytes 388
  75.2 7.7 %copy-start.6 = (f32[2]{0:T(128)S(1)}, f32[2]{0:T(128)}, u32[]{:S(2)}) copy-start(f32[2]{0:T(128)} %param.19) | copy-start | bytes 28
